TPU v7x, 128 devices: a whole 4x4x4 slice. The times are simulated.
128 devices in a mesh: freq: 16 (over z, y_lo, core), cell: 8 (over y_hi, x).
Axes of the slice: x: 4, y: 4 (y_hi: 2, y_lo: 2; y = y_hi * 2 + y_lo), z: 4, core: 2. Of those that a mesh axis runs over, the one named last changes fastest.
Arguments:
- covariance: bfloat16 [512, 2, 256, 256], P('freq', None, 'cell'), may hold values from -4 to 6, as said below
- replica: bfloat16 [512, 2, 256, 4096], P('freq', None, None, 'cell'), may hold values from -0.25 to 0.25
- transmission: bfloat16 [512, 4096], P('freq', 'cell'), may hold values from 0.29882812 to 3
Outputs:
- ambiguity: float32 [4096], P('cell')
- relative: float32 [4096], P('cell')
Inputs may be any that keep to these rules, and one draw needn't show every extreme that they name: Each covariance[f, 0] + i covariance[f, 1] is exactly Hermitian, also after rounding to bfloat16; before rounding all its eigenvalues are at least 0.5.
All inputs are finite; a program needn't handle non-finite values.
Results may differ from a plain program's by a relative error of at most 0.0003.
Values may be sent and summed in bfloat16 or wider, within the bound.
A program may use at most 384 MiB of HBM per device.

v0:
```python
import jax
import jax.numpy as jnp
from jax import lax
from jax.sharding import PartitionSpec as P


def copy_for_each(array, axis):
    copies = jnp.broadcast_to(array, (lax.axis_size(axis), *array.shape))
    return lax.all_to_all(copies, axis, split_axis=0, concat_axis=0, tiled=True)


def of_everyone(array, axis):
    return copy_for_each(array, axis).sum(axis=0)


def taken_together(array, axis):
    return copy_for_each(array, axis).max(axis=0)


def quadratic(cov_piece, col_fields, row_fields):
    count, _, rows, depths = cov_piece.shape
    stacked = cov_piece.reshape(count, 2 * rows, depths)
    first = jnp.einsum(
        "fij,fjc->fic", stacked, col_fields[:, 0], preferred_element_type=jnp.float32
    )
    second = jnp.einsum(
        "fij,fjc->fic", stacked, col_fields[:, 1], preferred_element_type=jnp.float32
    )
    image_re = first[:, :rows] - second[:, rows:]
    image_im = first[:, rows:] + second[:, :rows]
    return jnp.sum(row_fields[:, 0] * image_re + row_fields[:, 1] * image_im, axis=1)


def shards(covariance, replica, transmission):
    freq_total = covariance.shape[0] * lax.axis_size("freq")
    power = quadratic(lax.all_gather(covariance, "cell", axis=2, tiled=True), replica, replica)
    amplitude = transmission.astype(jnp.float32)
    partial_value = jnp.sum(amplitude * amplitude * power, axis=0)
    partial_value = partial_value / jnp.float32(freq_total)
    ambiguity = of_everyone(partial_value, "freq")
    peak = taken_together(jnp.max(ambiguity), "cell")
    relative = ambiguity / jnp.maximum(peak, jnp.float32(1.0))
    return (ambiguity, relative)


def solution(mesh):
    return jax.shard_map(
        shards,
        mesh=mesh,
        in_specs=(P("freq", None, "cell", None), P("freq", None, None, "cell"), P("freq", "cell")),
        out_specs=(P("cell"), P("cell")),
        check_vma=False,
    )
```

profile of v0, /device:TPU:1, one launch (start us, length us, event | category | flops | bytes accessed | tf_op | source)
XLA Modules:
  0.0 216.0 jit_solution(12335236490083693750)
XLA Ops:
  7.2 0.0 all-gather.2.cloned.1.call-start
  7.2 0.7 all-gather.2.cloned.1.call-update
  7.9 113.2 %all-gather.2.cloned.1.call-done = bf16[32,2,256,256]{3,2,1,0:T(8,128)(2,1)} async-done(((bf16[32,2,32,256]{3,2,1,0:T(8,128)(2,1)}), bf16[32,2,256,256]{3,2,1,0:T(8,128)(2,1)}) %all-gather.2.cloned.1.call-update) | async-done | bytes 8388624 | tf_op jit(solution)/shard_map/all_gather | solution.py:36
  121.1 17.7 %fusion.4 = f32[32,512,512]{2,1,0:T(8,128)} fusion(bf16[32,512,256]{2,1,0:T(8,128)(2,1)} %bitcast.15, bf16[32,2,256,512]{3,2,1,0:T(8,128)(2,1)} %param.4), kind=kOutput, calls=%fused_computation.6 | convolution fusion | flops 4294967296 | bytes 50331648 | tf_op jit(solution)/shard_map/fij,fjc->fic/dot_general | solution.py:26
  138.9 17.7 %fusion.6 = f32[32,512,512]{2,1,0:T(8,128)} fusion(bf16[32,512,256]{2,1,0:T(8,128)(2,1)} %bitcast.16, bf16[32,2,256,512]{3,2,1,0:T(8,128)(2,1)} %param.4), kind=kOutput, calls=%fused_computation.8 | convolution fusion | flops 4294967296 | bytes 50331648 | tf_op jit(solution)/shard_map/fij,fjc->fic/dot_general | solution.py:23
  156.6 0.0 copy-start
  156.6 27.6 %fusion.2 = f32[32,512]{1,0:T(8,128)S(1)} fusion(f32[32,512,512]{2,1,0:T(8,128)} %fusion.4, f32[32,512,512]{2,1,0:T(8,128)} %fusion.6, bf16[32,2,256,512]{3,2,1,0:T(8,128)(2,1)} %param.4), kind=kLoop, calls=%fused_computation.3 | loop fusion | flops 33538048 | bytes 83951616 | tf_op jit(solution)/shard_map/reduce_sum | solution.py:31
  184.2 0.0 copy-done
  184.3 11.5 %all_to_all.12 = f32[16,1,512]{2,1,0:T(1,128)S(1)} all-to-all(f32[16,1,512]{2,1,0:T(1,128)S(1)} %broadcast_in_dim.6), channel_id=1, replica_groups=mesh['freq'=16,'cell'=8] {'freq'}, dimensions={0} | all-to-all | bytes 65536 | tf_op jit(solution)/shard_map/all_to_all | solution.py:9
  195.8 0.0 copy-start.1
  195.8 0.6 reduce_max.18
  196.4 0.6 broadcast_in_dim.7
  197.0 10.3 %all_to_all.13 = f32[8,1,1]{2,1,0:T(1,128)S(1)} all-to-all(f32[8,1,1]{2,1,0:T(1,128)S(1)} %broadcast_in_dim.7), channel_id=1, replica_groups=mesh['freq'=16,'cell'=8] {'cell'}, dimensions={0} | all-to-all | bytes 64 | tf_op jit(solution)/shard_map/all_to_all | solution.py:9
  207.3 0.6 reduce_max.19
  208.6 0.6 broadcast_divide_fusion
  209.2 0.0 copy-done.1
  (4 shorter events, 0.1 us)
Async XLA Ops:
  7.2 114.0 %all-gather.2.cloned.1.call-start = ((), (), s32[]{:S(2)}) async-start(), calls=%async_computation.2 | async-start | bytes 9437184 | tf_op jit(solution)/shard_map/all_gather | solution.py:36
  156.6 27.6 %copy-start = (bf16[32,512]{1,0:T(8,128)(2,1)S(1)}, bf16[32,512]{1,0:T(8,128)(2,1)}, u32[]{:S(2)}) copy-start(bf16[32,512]{1,0:T(8,128)(2,1)} %param.5) | copy-start | bytes 98308
  195.8 13.4 %copy-start.1 = (f32[512]{0:T(512)}, f32[512]{0:T(512)S(1)}, u32[]{:S(2)}) copy-start(f32[512]{0:T(512)S(1)} %reduce_sum.29) | copy-start | bytes 6148
Sparse Core Ops, SparseCore 0:
  10.3 110.7 all-gather.1
where the time goes:
time: 217 us; the launch traced here: 216 us
  waiting for transfers between devices  114 us (53%)
  matrix products  35.5 us (16%)
  other arithmetic  29.5 us (14%)
  blocking collectives  21.7 us (10%)
  between operations  14.7 us (7%)
    all_gather x1, waiting for transfers between devices, shards(): lax.all_gather(covariance, 'cell', axis=2, tiled=True)  113 us
    reduce_sum x1, other arithmetic, quadratic(): jnp.sum(row_fields[:, 0] * image_re + row_fields[:, 1] * image_im, axis=1)  27.6 us
    all_to_all x2, blocking collectives, copy_for_each(): return lax.all_to_all(copies, axis, split_axis=0, concat_axis=0, tiled=True)  21.7 us
    dot_general x1, matrix products, quadratic(): jnp.einsum('fij,fjc->fic', stacked, col_fields[:, 1], preferred_element_t...  17.7 us
    dot_general x1, matrix products, quadratic(): jnp.einsum('fij,fjc->fic', stacked, col_fields[:, 0], preferred_element_t...  17.7 us
  transfers between devices with their start and end apart: 1, of which 1 were waited for; matrix products, arithmetic and copies ran while one was open for 0% of the time, Pallas kernels for 0%

commit v1 on v0

v1 whole, which is shorter than its diff:
```python
import functools

import jax
import jax.numpy as jnp
from jax import lax
from jax.experimental import pallas as pl
from jax.experimental.pallas import tpu as pltpu
from jax.sharding import PartitionSpec as P

MESH = pl.DeviceIdType.MESH
CHUNKS = ((4, "x"), (4, "y"), (4, "x"), (4, "y"), (4, "x"), (4, "y"), (4, "x"), (4, "x"))
AHEAD = 2
KINDS = 9


def kernel(
    cov_hbm, rep_hbm, trans_hbm, out_ref,
    diag, gathered, field, trans, weight, matrix, acc, sums, peaks,
    load_sem, rep_sem, send_sem, recv_sem, sum_send, sum_recv, peak_send, peak_recv,
):
    freq, cell = lax.axis_index("freq"), lax.axis_index("cell")
    n_freq, n_cell = lax.axis_size("freq"), lax.axis_size("cell")
    ring = n_cell // 2
    x, row = lax.rem(cell, ring), lax.div(cell, ring)

    def at(shift, other=False):
        r = 1 - row if other else row
        return r * ring + lax.rem(x + shift + ring, ring)

    lanes = gathered.shape[-1]
    own = pl.ds(pl.multiple_of(row * lanes, lanes), lanes)
    far = pl.ds(pl.multiple_of((1 - row) * lanes, lanes), lanes)
    diag_load = pltpu.make_async_copy(cov_hbm.at[:, :, :, own], diag, load_sem.at[0])
    far_load = pltpu.make_async_copy(
        cov_hbm.at[:, row, :, far], gathered.at[cell, :, 1], load_sem.at[1]
    )
    trans_load = pltpu.make_async_copy(trans_hbm, trans, load_sem.at[2])
    diag_load.start()
    far_load.start()
    trans_load.start()
    starts = [sum(c[0] for c in CHUNKS[:i]) for i in range(len(CHUNKS))]
    loads = []
    for i, (size, _) in enumerate(CHUNKS):
        part = pl.ds(starts[i], size)
        loads.append(pltpu.make_async_copy(rep_hbm.at[part], field.at[part], rep_sem.at[i]))
        loads[-1].start()

    barrier = pltpu.get_barrier_semaphore()
    for step in range(1, n_freq):
        pl.semaphore_signal(
            barrier, inc=1, device_id={"freq": lax.rem(freq + step, n_freq)}, device_id_type=MESH
        )
    for step in range(1, n_cell):
        pl.semaphore_signal(
            barrier, inc=1, device_id={"cell": lax.rem(cell + step, n_cell)}, device_id_type=MESH
        )

    diag_load.wait()
    shape = diag.shape[2:]
    line = lax.broadcasted_iota(jnp.int32, shape, 0) + x * shape[0]
    column = lax.broadcasted_iota(jnp.int32, shape, 1)
    factor = jnp.where(line == column, 0.5, 1.0).astype(jnp.float32)
    above = line <= column

    def pack(f, carry):
        re = diag[f, 0].astype(jnp.float32) * factor
        im = diag[f, 1].astype(jnp.float32)
        gathered[cell, f, 0] = jnp.where(above, re, im).astype(jnp.bfloat16)
        return carry

    lax.fori_loop(0, diag.shape[0], pack, 0, unroll=4)
    trans_load.wait()
    amplitude = trans[...].astype(jnp.float32)
    weight[...] = amplitude * amplitude
    acc[...] = jnp.zeros_like(acc)
    far_load.wait()
    pl.semaphore_wait(barrier, n_freq + n_cell - 2)

    def send(chunk, kind, piece, target, half=None):
        size = CHUNKS[chunk][0]
        first = starts[chunk]
        if half is not None:
            size //= 2
            first += half * size
        ref = gathered.at[piece, pl.ds(first, size)]
        copy = pltpu.make_async_remote_copy(
            src_ref=ref, dst_ref=ref,
            send_sem=send_sem.at[chunk, kind], recv_sem=recv_sem.at[chunk, kind],
            device_id={"cell": target}, device_id_type=MESH,
        )
        copy.start()
        return copy

    right, left, partner = at(1), at(-1), at(0, True)
    chunks = len(CHUNKS)
    zero = [None] * chunks
    one = [None] * chunks
    two = [None] * chunks

    def issue_zero(c):
        zero[c] = (
            send(c, 2, cell, partner), send(c, 0, cell, right), send(c, 1, cell, left),
        )

    def issue_one(c):
        to_partner, to_right, to_left = zero[c]
        if CHUNKS[c][1] == "x":
            to_right.wait_recv()
            a = send(c, 5, left, right, 0)
            to_left.wait_recv()
            b = send(c, 6, right, left, 1)
            to_partner.wait_recv()
            one[c] = (a, b, send(c, 3, partner, right), send(c, 4, partner, left))
        else:
            to_right.wait_recv()
            a = send(c, 5, left, right, 0)
            d = send(c, 3, left, partner)
            to_left.wait_recv()
            b = send(c, 6, right, left, 1)
            e = send(c, 4, right, partner)
            to_partner.wait_recv()
            one[c] = (a, b, d, e)

    def issue_two(c):
        a, b, d, e = one[c]
        if CHUNKS[c][1] == "x":
            d.wait_recv()
            g = send(c, 7, at(-1, True), right, 0)
            e.wait_recv()
            h = send(c, 8, at(1, True), left, 1)
            a.wait_recv()
            b.wait_recv()
            two[c] = (g, h)
        else:
            a.wait_recv()
            b.wait_recv()
            two[c] = (send(c, 7, at(2), partner),)
            d.wait_recv()
            e.wait_recv()

    half = lanes
    tri_line = lax.broadcasted_iota(jnp.int32, (half, half), 0)
    tri_column = lax.broadcasted_iota(jnp.int32, (half, half), 1)
    upper = tri_line <= tri_column
    blank = jnp.zeros((half, half), jnp.bfloat16)
    depth2 = field.shape[1] * field.shape[2]
    cells = field.shape[3]

    def block(first, f, part):
        return gathered[pl.ds(first, ring), f, part].reshape(half, half)

    matrix[pl.ds(0, half), pl.ds(3 * half, half)] = blank
    matrix[pl.ds(half, half), pl.ds(0, half)] = blank
    matrix[pl.ds(2 * half, half), pl.ds(half, half)] = blank
    matrix[pl.ds(3 * half, half), pl.ds(2 * half, half)] = blank

    def put(i, j, value):
        matrix[pl.ds(i * half, half), pl.ds(j * half, half)] = value

    def one_frequency(f, carry):
        for b in range(2):
            packed = block(b * ring, f, 0).astype(jnp.float32)
            sym = jnp.where(upper, packed, 0.0).astype(jnp.bfloat16)
            skew = jnp.where(upper, 0.0, packed)
            put(b, b, sym)
            put(2 + b, 2 + b, sym)
            put(2 + b, b, skew.astype(jnp.bfloat16))
            put(b, 2 + b, (-skew).astype(jnp.bfloat16))
        across = block(0, f, 1)
        put(0, 1, across)
        put(2, 3, across)
        below = block(ring, f, 1)
        put(3, 0, below)
        put(1, 2, -below)
        v = field[f].reshape(depth2, cells)
        image = jnp.dot(matrix[...], v, preferred_element_type=jnp.float32)
        power = jnp.sum((v.astype(jnp.float32) * image).reshape(depth2 // 8, 8, cells), axis=0)
        acc[...] += power * weight[pl.ds(f, 1), :]
        return carry

    def compute(c):
        for copy in two[c]:
            copy.wait_recv()
        loads[c].wait()
        lax.fori_loop(starts[c], starts[c] + CHUNKS[c][0], one_frequency, 0)

    for c in range(min(AHEAD, chunks)):
        issue_zero(c)
    for step in range(chunks + 2):
        if step < chunks:
            issue_one(step)
            if step + AHEAD < chunks:
                issue_zero(step + AHEAD)
        if 0 <= step - 1 < chunks:
            issue_two(step - 1)
        if 0 <= step - 2 < chunks:
            compute(step - 2)

    total = 2.0 / (n_freq * field.shape[0])
    sums[freq] = jnp.sum(acc[...], axis=0, keepdims=True) * total
    for c in range(chunks):
        for copy in (*zero[c], *one[c], *two[c]):
            copy.wait_send()
    copies = []
    for step in range(1, n_freq):
        copies.append(pltpu.make_async_remote_copy(
            src_ref=sums.at[freq], dst_ref=sums.at[freq],
            send_sem=sum_send.at[step], recv_sem=sum_recv.at[step],
            device_id={"freq": lax.rem(freq + step, n_freq)}, device_id_type=MESH,
        ))
        copies[-1].start()
    for copy in copies:
        copy.wait_recv()
    ambiguity = jnp.sum(sums[...], axis=0)
    peak = jnp.max(ambiguity, axis=1, keepdims=True)
    peaks[cell] = jnp.broadcast_to(peak, peaks.shape[1:])
    for copy in copies:
        copy.wait_send()
    copies = []
    for step in range(1, n_cell):
        copies.append(pltpu.make_async_remote_copy(
            src_ref=peaks.at[cell], dst_ref=peaks.at[cell],
            send_sem=peak_send.at[step], recv_sem=peak_recv.at[step],
            device_id={"cell": lax.rem(cell + step, n_cell)}, device_id_type=MESH,
        ))
        copies[-1].start()
    out_ref[0:1, :] = ambiguity
    for copy in copies:
        copy.wait_recv()
    top = jnp.max(jnp.max(peaks[...], axis=0), axis=1, keepdims=True)
    out_ref[1:2, :] = ambiguity / jnp.maximum(top, 1.0)
    for copy in copies:
        copy.wait_send()


def shards(covariance, replica, transmission):
    freqs, _, rows, depth = covariance.shape
    cells = replica.shape[3]
    n_freq, n_cell = lax.axis_size("freq"), lax.axis_size("cell")
    out = pl.pallas_call(
        kernel,
        out_shape=jax.ShapeDtypeStruct((2, cells), jnp.float32),
        in_specs=[pl.BlockSpec(memory_space=pltpu.HBM)] * 3,
        out_specs=pl.BlockSpec(memory_space=pltpu.VMEM),
        scratch_shapes=[
            pltpu.VMEM((freqs, 2, rows, depth // 2), jnp.bfloat16),
            pltpu.VMEM((n_cell, freqs, 2, rows, depth // 2), jnp.bfloat16),
            pltpu.VMEM((freqs, 2, depth, cells), jnp.bfloat16),
            pltpu.VMEM((freqs, cells), jnp.bfloat16),
            pltpu.VMEM((freqs, cells), jnp.float32),
            pltpu.VMEM((2 * depth, 2 * depth), jnp.bfloat16),
            pltpu.VMEM((8, cells), jnp.float32),
            pltpu.VMEM((n_freq, 1, cells), jnp.float32),
            pltpu.VMEM((n_cell, 1, 128), jnp.float32),
            pltpu.SemaphoreType.DMA((3,)),
            pltpu.SemaphoreType.DMA((len(CHUNKS),)),
            pltpu.SemaphoreType.DMA((len(CHUNKS), KINDS)),
            pltpu.SemaphoreType.DMA((len(CHUNKS), KINDS)),
            pltpu.SemaphoreType.DMA((n_freq,)),
            pltpu.SemaphoreType.DMA((n_freq,)),
            pltpu.SemaphoreType.DMA((n_cell,)),
            pltpu.SemaphoreType.DMA((n_cell,)),
        ],
        compiler_params=pltpu.CompilerParams(collective_id=0, has_side_effects=True),
    )(covariance, replica, transmission)
    return out[0], out[1]


def solution(mesh):
    return jax.shard_map(
        shards,
        mesh=mesh,
        in_specs=(P("freq", None, "cell", None), P("freq", None, None, "cell"), P("freq", "cell")),
        out_specs=(P("cell"), P("cell")),
        check_vma=False,
    )
```

time: 217 us -> 62.5 us (0.29)
  waiting for transfers between devices: 114 us -> 0 us
  Pallas kernels: 0 us -> 60.4 us
  matrix products: 35.5 us -> 0 us
  other arithmetic: 29.5 us -> 0 us
  blocking collectives: 21.7 us -> 0 us
  between operations: 14.7 us -> 0.64 us
    all_gather x1 -> x0, waiting for transfers between devices: 113 us -> none  [shards(): lax.all_gather(covariance, 'cell', axis=2, tiled=True)]
    pallas_call x0 -> x1, Pallas kernels: none -> 60.4 us  [shards(): pl.pallas_call(kernel, out_shape=jax.ShapeDtypeStruct((2, cells), jnp.flo...]
    dot_general x2 -> x0, matrix products: 35.5 us -> none  [the longest x1 17.7 us: quadratic(): jnp.einsum('fij,fjc->fic', stacked, col_fields[:, 1], preferred_element_t...]
    reduce_sum x3 -> x0, other arithmetic: 27.7 us -> none  [the longest x1 27.6 us: quadratic(): jnp.sum(row_fields[:, 0] * image_re + row_fields[:, 1] * image_im, axis=1)]
    all_to_all x2 -> x0, blocking collectives: 21.7 us -> none  [copy_for_each(): return lax.all_to_all(copies, axis, split_axis=0, concat_axis=0, tiled=True)]
  transfers between devices with their start and end apart: 1 -> 0, of which waited for: 1 -> 0; matrix products, arithmetic and copies ran while one was open for 0% -> 0% of each run, Pallas kernels for 0% -> 0%
where the time goes in v1:
time: 62.5 us; the launch traced here: 62.4 us
  Pallas kernels  60.4 us (97%)
  local copies, waits for them, and re-layouts  1.33 us (2%)
  between operations  0.64 us (1%)
    pallas_call x1, Pallas kernels, shards(): pl.pallas_call(kernel, out_shape=jax.ShapeDtypeStruct((2, cells), jnp.flo...  60.4 us
    slice x1, local copies, waits for them, and re-layouts, shards(): return (out[0], out[1])  1.33 us

profile of v1, /device:TPU:1, one launch (start us, length us, event | category | flops | bytes accessed | tf_op | source)
XLA Modules:
  0.0 62.4 jit_solution(16892389664755719541)
XLA Ops:
  0.6 60.4 %shard_map.50 = f32[2,512]{1,0:T(2,128)} custom-call(bf16[32,2,32,256]{3,2,1,0:T(8,128)(2,1)} %cov_hbm.1, bf16[32,2,256,512]{3,2,1,0:T(8,128)(2,1)} %rep_hbm.1, bf16[32,512]{1,0:T(8,128)(2,1)} %trans_hbm.1), custom_call_target="tpu_custom_call" | custom-call | tf_op jit(solution)/shard_map/pallas_call | solution.py:240
  61.0 1.3 %fusion = (f32[1,512]{1,0:T(1,128)}, f32[1,512]{1,0:T(1,128)}) fusion(f32[2,512]{1,0:T(2,128)} %shard_map.50), kind=kLoop, calls=%fused_computation | loop fusion | bytes 8192 | tf_op jit(solution)/shard_map/slice | solution.py:266

commit v2 on v0

v2 whole, which is shorter than its diff:
```python
import functools

import jax
import jax.numpy as jnp
from jax import lax
from jax.experimental import pallas as pl
from jax.experimental.pallas import tpu as pltpu
from jax.sharding import PartitionSpec as P

MESH = pl.DeviceIdType.MESH
CHUNKS = 8
PATTERN = ((2, 2), (3, 1), (2, 2), (2, 2))
AHEAD = 3
SECOND = 2
THIRD = 5
KINDS = 12


def kernel(
    cov_hbm, rep_hbm, trans_hbm, out_ref,
    diag, gathered, field, trans, weight, matrix, acc, sums, peaks,
    load_sem, rep_sem, send_sem, recv_sem, sum_send, sum_recv, peak_send, peak_recv,
):
    freq, cell = lax.axis_index("freq"), lax.axis_index("cell")
    n_freq, n_cell = lax.axis_size("freq"), lax.axis_size("cell")
    ring = n_cell // 2
    x, row = lax.rem(cell, ring), lax.div(cell, ring)

    def at(shift, other=False):
        r = 1 - row if other else row
        return r * ring + lax.rem(x + shift + ring, ring)

    lanes = gathered.shape[-1]
    own = pl.ds(pl.multiple_of(row * lanes, lanes), lanes)
    far = pl.ds(pl.multiple_of((1 - row) * lanes, lanes), lanes)
    diag_load = pltpu.make_async_copy(cov_hbm.at[:, :, :, own], diag, load_sem.at[0])
    far_load = pltpu.make_async_copy(
        cov_hbm.at[:, row, :, far], gathered.at[cell, :, 1], load_sem.at[1]
    )
    trans_load = pltpu.make_async_copy(trans_hbm, trans, load_sem.at[2])
    diag_load.start()
    far_load.start()
    trans_load.start()
    period = len(PATTERN)
    offsets = [sum(sum(p) for p in PATTERN[:i]) for i in range(period + 1)]

    def load(c, k):
        part = pl.ds(lax.div(c, period) * offsets[-1] + offsets[k], sum(PATTERN[k]))
        return pltpu.make_async_copy(rep_hbm.at[part], field.at[part], rep_sem.at[c])

    def load_one(i, carry):
        for k in range(period):
            load(i * period + k, k).start()
        return carry

    lax.fori_loop(0, CHUNKS // period, load_one, 0)

    barrier = pltpu.get_barrier_semaphore()
    def greet(axis, me, n):
        def one(step, carry):
            pl.semaphore_signal(
                barrier, inc=1, device_id={axis: lax.rem(me + step, n)}, device_id_type=MESH
            )
            return carry

        lax.fori_loop(1, n, one, 0)

    greet("freq", freq, n_freq)
    greet("cell", cell, n_cell)

    diag_load.wait()
    shape = diag.shape[2:]
    line = lax.broadcasted_iota(jnp.int32, shape, 0) + x * shape[0]
    column = lax.broadcasted_iota(jnp.int32, shape, 1)
    factor = jnp.where(line == column, 0.5, 1.0).astype(jnp.float32)
    above = line <= column

    def pack(f, carry):
        re = diag[f, 0].astype(jnp.float32) * factor
        im = diag[f, 1].astype(jnp.float32)
        gathered[cell, f, 0] = jnp.where(above, re, im).astype(jnp.bfloat16)
        return carry

    lax.fori_loop(0, diag.shape[0], pack, 0, unroll=4)
    trans_load.wait()
    amplitude = trans[...].astype(jnp.float32)
    weight[...] = amplitude * amplitude
    acc[...] = jnp.zeros_like(acc)
    far_load.wait()
    pl.semaphore_wait(barrier, n_freq + n_cell - 2)

    right, left, partner = at(1), at(-1), at(0, True)
    TO_PARTNER, TO_RIGHT, TO_LEFT = 0, 1, 2
    ON_RIGHT, LEFT_OVER, ON_LEFT, RIGHT_OVER, OTHER_RIGHT, OTHER_LEFT = 3, 4, 5, 6, 7, 8
    FAR_OVER, OTHER_ON_RIGHT, OTHER_ON_LEFT = 9, 10, 11

    def kinds(k):
        by_x, by_y = PATTERN[k]
        size = by_x + by_y
        mid, mid_x = (size + k % 2) // 2, (by_x + 1 - k % 2) // 2
        table = {
            TO_PARTNER: (cell, partner, 0, size),
            TO_RIGHT: (cell, right, 0, size),
            TO_LEFT: (cell, left, 0, size),
            ON_RIGHT: (left, right, 0, mid),
            LEFT_OVER: (left, partner, by_x, by_y),
            ON_LEFT: (right, left, mid, size - mid),
            RIGHT_OVER: (right, partner, by_x, by_y),
            OTHER_RIGHT: (partner, right, 0, by_x),
            OTHER_LEFT: (partner, left, 0, by_x),
            FAR_OVER: (at(2), partner, by_x, by_y),
            OTHER_ON_RIGHT: (at(-1, True), right, 0, mid_x),
            OTHER_ON_LEFT: (at(1, True), left, mid_x, by_x - mid_x),
        }
        return {kind: row for kind, row in table.items() if row[3]}

    def copy_of(c, k, kind):
        piece, target, first, size = kinds(k)[kind]
        begin = lax.div(c, period) * offsets[-1] + offsets[k] + first
        ref = gathered.at[piece, pl.ds(begin, size)]
        return pltpu.make_async_remote_copy(
            src_ref=ref, dst_ref=ref,
            send_sem=send_sem.at[c, kind], recv_sem=recv_sem.at[c, kind],
            device_id={"cell": target}, device_id_type=MESH,
        )

    def start(c, k, *wanted):
        for kind in wanted:
            if kind in kinds(k):
                copy_of(c, k, kind).start()

    def arrived(c, k, *wanted):
        for kind in wanted:
            if kind in kinds(k):
                copy_of(c, k, kind).wait_recv()

    def issue_zero(c, k):
        start(c, k, TO_PARTNER, TO_RIGHT, TO_LEFT)

    def issue_one(c, k):
        arrived(c, k, TO_RIGHT)
        start(c, k, ON_RIGHT, LEFT_OVER)
        arrived(c, k, TO_LEFT)
        start(c, k, ON_LEFT, RIGHT_OVER)
        arrived(c, k, TO_PARTNER)
        start(c, k, OTHER_RIGHT, OTHER_LEFT)

    def issue_two(c, k):
        arrived(c, k, ON_RIGHT, ON_LEFT)
        start(c, k, FAR_OVER)
        arrived(c, k, OTHER_RIGHT)
        start(c, k, OTHER_ON_RIGHT)
        arrived(c, k, OTHER_LEFT)
        start(c, k, OTHER_ON_LEFT)
        arrived(c, k, LEFT_OVER, RIGHT_OVER)

    half = lanes
    tri_line = lax.broadcasted_iota(jnp.int32, (half, half), 0)
    tri_column = lax.broadcasted_iota(jnp.int32, (half, half), 1)
    upper = tri_line <= tri_column
    blank = jnp.zeros((half, half), jnp.bfloat16)
    depth2 = field.shape[1] * field.shape[2]
    cells = field.shape[3]

    def block(first, f, part):
        return gathered[pl.ds(first, ring), f, part].reshape(half, half)

    for slot in range(2):
        for i, j in ((0, 3), (1, 0), (2, 1), (3, 2)):
            matrix[slot, pl.ds(i * half, half), pl.ds(j * half, half)] = blank

    def one_frequency(f, slot):
        def put(i, j, value):
            matrix[slot, pl.ds(i * half, half), pl.ds(j * half, half)] = value

        for b in range(2):
            packed = block(b * ring, f, 0)
            sym = jnp.where(upper, packed, blank)
            skew = jnp.where(upper, blank, packed)
            put(b, b, sym)
            put(2 + b, 2 + b, sym)
            put(2 + b, b, skew)
            put(b, 2 + b, -skew)
        across = block(0, f, 1)
        put(0, 1, across)
        put(2, 3, across)
        below = block(ring, f, 1)
        put(3, 0, below)
        put(1, 2, -below)
        v = field[f].reshape(depth2, cells)
        image = jnp.dot(matrix[slot], v, preferred_element_type=jnp.float32)
        power = jnp.sum((v.astype(jnp.float32) * image).reshape(depth2 // 8, 8, cells), axis=0)
        return power * weight[pl.ds(f, 1), :]

    def compute(c, k, second):
        if not second:
            arrived(c, k, FAR_OVER, OTHER_ON_RIGHT, OTHER_ON_LEFT)
            load(c, k).wait()
        size = sum(PATTERN[k])
        half_size = size // 2
        f = lax.div(c, period) * offsets[-1] + offsets[k] + second * half_size
        if half_size == 1:
            acc[...] += one_frequency(f, 0)
        else:
            acc[...] += one_frequency(f, 0) + one_frequency(f + 1, 1)

    for c in range(AHEAD):
        issue_zero(c, c % period)

    def steps(i, carry):
        for k in range(period):
            step = i * period + k

            @pl.when(step + AHEAD < CHUNKS)
            def _():
                issue_zero(step + AHEAD, (k + AHEAD) % period)

            @pl.when(step < CHUNKS)
            def _():
                issue_one(step, k)

            @pl.when(jnp.logical_and(step >= THIRD, step - THIRD < CHUNKS))
            def _():
                compute(step - THIRD, (k - THIRD) % period, 0)

            @pl.when(jnp.logical_and(step >= SECOND, step - SECOND < CHUNKS))
            def _():
                issue_two(step - SECOND, (k - SECOND) % period)

            @pl.when(jnp.logical_and(step >= THIRD, step - THIRD < CHUNKS))
            def _():
                compute(step - THIRD, (k - THIRD) % period, 1)

        return carry

    lax.fori_loop(0, -(-(CHUNKS + THIRD) // period), steps, 0)

    def spread(ref, axis, me, n, ssem, rsem):
        def copy(step):
            return pltpu.make_async_remote_copy(
                src_ref=ref.at[me], dst_ref=ref.at[me],
                send_sem=ssem.at[step], recv_sem=rsem.at[step],
                device_id={axis: lax.rem(me + step, n)}, device_id_type=MESH,
            )

        def each(act):
            def one(step, carry):
                act(copy(step))
                return carry

            return lambda: lax.fori_loop(1, n, one, 0)

        return (
            each(lambda c: c.start()), each(lambda c: c.wait_recv()), each(lambda c: c.wait_send())
        )

    def sent(i, carry):
        for k in range(period):
            for kind in kinds(k):
                copy_of(i * period + k, k, kind).wait_send()
        return carry

    total = 2.0 / (n_freq * field.shape[0])
    sums[freq] = jnp.sum(acc[...], axis=0, keepdims=True) * total
    go, got, gone = spread(sums, "freq", freq, n_freq, sum_send, sum_recv)
    go()
    lax.fori_loop(0, CHUNKS // period, sent, 0)
    got()
    ambiguity = jnp.sum(sums[...], axis=0)
    peak = jnp.max(ambiguity, axis=1, keepdims=True)
    peaks[cell] = jnp.broadcast_to(peak, peaks.shape[1:])
    go_peak, got_peak, gone_peak = spread(peaks, "cell", cell, n_cell, peak_send, peak_recv)
    go_peak()
    gone()
    out_ref[0:1, :] = ambiguity
    got_peak()
    top = jnp.max(jnp.max(peaks[...], axis=0), axis=1, keepdims=True)
    out_ref[1:2, :] = ambiguity / jnp.maximum(top, 1.0)
    gone_peak()


def shards(covariance, replica, transmission):
    freqs, _, rows, depth = covariance.shape
    cells = replica.shape[3]
    n_freq, n_cell = lax.axis_size("freq"), lax.axis_size("cell")
    out = pl.pallas_call(
        kernel,
        out_shape=jax.ShapeDtypeStruct((2, cells), jnp.float32),
        in_specs=[pl.BlockSpec(memory_space=pltpu.HBM)] * 3,
        out_specs=pl.BlockSpec(memory_space=pltpu.VMEM),
        scratch_shapes=[
            pltpu.VMEM((freqs, 2, rows, depth // 2), jnp.bfloat16),
            pltpu.VMEM((n_cell, freqs, 2, rows, depth // 2), jnp.bfloat16),
            pltpu.VMEM((freqs, 2, depth, cells), jnp.bfloat16),
            pltpu.VMEM((freqs, cells), jnp.bfloat16),
            pltpu.VMEM((freqs, cells), jnp.float32),
            pltpu.VMEM((2, 2 * depth, 2 * depth), jnp.bfloat16),
            pltpu.VMEM((8, cells), jnp.float32),
            pltpu.VMEM((n_freq, 1, cells), jnp.float32),
            pltpu.VMEM((n_cell, 1, 128), jnp.float32),
            pltpu.SemaphoreType.DMA((3,)),
            pltpu.SemaphoreType.DMA((CHUNKS,)),
            pltpu.SemaphoreType.DMA((CHUNKS, KINDS)),
            pltpu.SemaphoreType.DMA((CHUNKS, KINDS)),
            pltpu.SemaphoreType.DMA((n_freq,)),
            pltpu.SemaphoreType.DMA((n_freq,)),
            pltpu.SemaphoreType.DMA((n_cell,)),
            pltpu.SemaphoreType.DMA((n_cell,)),
        ],
        compiler_params=pltpu.CompilerParams(collective_id=0, has_side_effects=True, vmem_limit_bytes=40 * 2**20),
    )(*[pltpu.with_memory_space_constraint(a, pltpu.HBM) for a in (covariance, replica, transmission)])
    return out[0], out[1]


def solution(mesh):
    return jax.shard_map(
        shards,
        mesh=mesh,
        in_specs=(P("freq", None, "cell", None), P("freq", None, None, "cell"), P("freq", "cell")),
        out_specs=(P("cell"), P("cell")),
        check_vma=False,
    )
```

time: 217 us -> 54.6 us (0.25)
  waiting for transfers between devices: 114 us -> 0 us
  Pallas kernels: 0 us -> 53.3 us
  matrix products: 35.5 us -> 0 us
  other arithmetic: 29.5 us -> 0 us
  blocking collectives: 21.7 us -> 0 us
  between operations: 14.7 us -> 0.64 us
    all_gather x1 -> x0, waiting for transfers between devices: 113 us -> none  [shards(): lax.all_gather(covariance, 'cell', axis=2, tiled=True)]
    pallas_call x0 -> x1, Pallas kernels: none -> 53.3 us  [shards(): pl.pallas_call(kernel, out_shape=jax.ShapeDtypeStruct((2, cells), jnp.flo...]
    dot_general x2 -> x0, matrix products: 35.5 us -> none  [the longest x1 17.7 us: quadratic(): jnp.einsum('fij,fjc->fic', stacked, col_fields[:, 1], preferred_element_t...]
    reduce_sum x3 -> x0, other arithmetic: 27.7 us -> none  [the longest x1 27.6 us: quadratic(): jnp.sum(row_fields[:, 0] * image_re + row_fields[:, 1] * image_im, axis=1)]
    all_to_all x2 -> x0, blocking collectives: 21.7 us -> none  [copy_for_each(): return lax.all_to_all(copies, axis, split_axis=0, concat_axis=0, tiled=True)]
  transfers between devices with their start and end apart: 1 -> 0, of which waited for: 1 -> 0; matrix products, arithmetic and copies ran while one was open for 0% -> 0% of each run, Pallas kernels for 0% -> 0%
where the time goes in v2:
time: 54.6 us; the launch traced here: 54.5 us
  Pallas kernels  53.3 us (98%)
  between operations  0.64 us (1%)
  local copies, waits for them, and re-layouts  0.59 us (1%)
    pallas_call x1, Pallas kernels, shards(): pl.pallas_call(kernel, out_shape=jax.ShapeDtypeStruct((2, cells), jnp.flo...  53.3 us

profile of v2, /device:TPU:1, one launch (start us, length us, event | category | flops | bytes accessed | tf_op | source)
XLA Modules:
  0.0 54.5 jit_solution(5642220186647195719)
XLA Ops:
  0.6 53.3 %shard_map.50 = f32[2,512]{1,0:T(2,128)S(1)} custom-call(bf16[32,2,32,256]{3,2,1,0:T(8,128)(2,1)} %cov_hbm.1, bf16[32,2,256,512]{3,2,1,0:T(8,128)(2,1)} %rep_hbm.1, bf16[32,512]{1,0:T(8,128)(2,1)} %trans_hbm.1), custom_call_target="tpu_custom_call" | custom-call | tf_op jit(solution)/shard_map/pallas_call | solution.py:286
  53.9 0.6 %fusion = (f32[1,512]{1,0:T(1,128)}, f32[1,512]{1,0:T(1,128)}) fusion(f32[2,512]{1,0:T(2,128)S(1)} %shard_map.50), kind=kLoop, calls=%fused_computation | loop fusion | bytes 8192 | tf_op jit(solution)/shard_map/slice | solution.py:312

commit v3 on v0

v3 whole, which is shorter than its diff:
```python
import functools

import jax
import jax.numpy as jnp
from jax import lax
from jax.experimental import pallas as pl
from jax.experimental.pallas import tpu as pltpu
from jax.sharding import PartitionSpec as P

MESH = pl.DeviceIdType.MESH
CHUNKS = 8
PIECES = 16
BY_X = 9
AHEAD = 3
SECOND = 2
THIRD = 5
KINDS = 12
CORES, Y_LOW = 2, 2


def kernel(
    cov_hbm, rep_hbm, trans_hbm, out_ref,
    diag, far, gathered, field, trans, weight, matrix, acc, sums, parts,
    load_sem, rep_sem, send_sem, recv_sem, sum_send, sum_recv, part_send, part_recv, word,
):
    freq, cell = lax.axis_index("freq"), lax.axis_index("cell")
    n_cell = lax.axis_size("cell")
    ring = n_cell // 2
    x, row = lax.rem(cell, ring), lax.div(cell, ring)

    def at(shift, other=False):
        r = 1 - row if other else row
        return r * ring + lax.rem(x + shift + ring, ring)

    lanes = gathered.shape[-1]
    freqs = field.shape[0]
    per_freq = gathered.shape[1] // freqs
    size = freqs // CHUNKS
    own = pl.ds(pl.multiple_of(row * lanes, lanes), lanes)
    other = pl.ds(pl.multiple_of((1 - row) * lanes, lanes), lanes)
    row_loads = []
    for i, part in enumerate((pl.ds(0, size), pl.ds(size, freqs - size))):
        row_loads.append((
            pltpu.make_async_copy(cov_hbm.at[part, :, :, own], diag.at[part], load_sem.at[2 * i]),
            pltpu.make_async_copy(
                cov_hbm.at[part, row, :, other], far.at[part], load_sem.at[2 * i + 1]
            ),
        ))
        for copy in row_loads[-1]:
            copy.start()
    trans_load = pltpu.make_async_copy(trans_hbm, trans, load_sem.at[4])
    trans_load.start()

    def load(c):
        part = pl.ds(c * size, size)
        return pltpu.make_async_copy(rep_hbm.at[part], field.at[part], rep_sem.at[c])

    def load_one(c, carry):
        load(c).start()
        return carry

    lax.fori_loop(0, CHUNKS, load_one, 0)

    core, y_low = lax.rem(freq, CORES), lax.rem(lax.div(freq, CORES), Y_LOW)
    z = lax.div(freq, CORES * Y_LOW)
    me_sum, n_sum = z * CORES + core, sums.shape[0]
    me_part, n_part = cell * Y_LOW + y_low, parts.shape[0]

    def sum_peer(step):
        j = lax.rem(me_sum + step, n_sum)
        return {"freq": (lax.div(j, CORES) * Y_LOW + y_low) * CORES + lax.rem(j, CORES)}

    def part_peer(step):
        j = lax.rem(me_part + step, n_part)
        return {
            "freq": (z * Y_LOW + lax.rem(j, Y_LOW)) * CORES + core, "cell": lax.div(j, Y_LOW)
        }

    barrier = pltpu.get_barrier_semaphore()

    n_z = n_sum // CORES
    freq_at = lambda zz, yy, cc: {"freq": (zz * Y_LOW + yy) * CORES + cc}
    neighbours = (
        {"cell": at(1)}, {"cell": at(-1)}, {"cell": at(0, True)},
        freq_at(z, y_low, 1 - core),
        freq_at(lax.rem(z + 1, n_z), y_low, core), freq_at(lax.rem(z + n_z - 1, n_z), y_low, core),
        freq_at(z, 1 - y_low, core),
        {**freq_at(z, 1 - y_low, core), "cell": at(0, True)},
    )

    def greet(semaphore):
        for target in neighbours:
            pl.semaphore_signal(semaphore, inc=1, device_id=target, device_id_type=MESH)

    greet(barrier)

    shape = diag.shape[2:]
    rows = shape[0] // 2
    line = lax.broadcasted_iota(jnp.int32, shape, 0) + x * shape[0]
    column = lax.broadcasted_iota(jnp.int32, shape, 1)
    factor = jnp.where(line == column, 0.5, 1.0).astype(jnp.bfloat16)
    above = line <= column

    def pack(f, carry):
        packed = jnp.where(above, diag[f, 0] * factor, diag[f, 1])
        across = far[f]
        for i in range(2):
            gathered[cell, per_freq * f + i] = packed[i * rows:(i + 1) * rows]
            gathered[cell, per_freq * f + 2 + i] = across[i * rows:(i + 1) * rows]
        return carry

    for copy in row_loads[0]:
        copy.wait()
    lax.fori_loop(0, size, pack, 0, unroll=4)

    right, left, partner = at(1), at(-1), at(0, True)
    TO_PARTNER, TO_RIGHT, TO_LEFT = 0, 1, 2
    ON_RIGHT, LEFT_OVER, ON_LEFT, RIGHT_OVER, OTHER_RIGHT, OTHER_LEFT = 3, 4, 5, 6, 7, 8
    FAR_OVER, OTHER_ON_RIGHT, OTHER_ON_LEFT = 9, 10, 11

    mid, mid_x, by_y = PIECES // 2, BY_X // 2, PIECES - BY_X
    table = {
        TO_PARTNER: (cell, partner, 0, PIECES),
        TO_RIGHT: (cell, right, 0, PIECES),
        TO_LEFT: (cell, left, 0, PIECES),
        ON_RIGHT: (left, right, 0, mid),
        LEFT_OVER: (left, partner, BY_X, by_y),
        ON_LEFT: (right, left, mid, PIECES - mid),
        RIGHT_OVER: (right, partner, BY_X, by_y),
        OTHER_RIGHT: (partner, right, 0, BY_X),
        OTHER_LEFT: (partner, left, 0, BY_X),
        FAR_OVER: (at(2), partner, BY_X, by_y),
        OTHER_ON_RIGHT: (at(-1, True), right, 0, mid_x),
        OTHER_ON_LEFT: (at(1, True), left, mid_x, BY_X - mid_x),
    }

    def copy_of(c, kind):
        source, target, first, count = table[kind]
        ref = gathered.at[source, pl.ds(c * PIECES + first, count)]
        return pltpu.make_async_remote_copy(
            src_ref=ref, dst_ref=ref,
            send_sem=send_sem.at[c, kind], recv_sem=recv_sem.at[c, kind],
            device_id={"cell": target}, device_id_type=MESH,
        )

    def start(c, *wanted):
        for kind in wanted:
            copy_of(c, kind).start()

    def arrived(c, *wanted):
        for kind in wanted:
            copy_of(c, kind).wait_recv()

    def issue_zero(c):
        start(c, TO_PARTNER, TO_RIGHT, TO_LEFT)

    def issue_one(c):
        arrived(c, TO_RIGHT)
        start(c, ON_RIGHT, LEFT_OVER)
        arrived(c, TO_LEFT)
        start(c, ON_LEFT, RIGHT_OVER)
        arrived(c, TO_PARTNER)
        start(c, OTHER_RIGHT, OTHER_LEFT)

    def issue_two(c):
        arrived(c, ON_RIGHT, ON_LEFT)
        start(c, FAR_OVER)
        arrived(c, OTHER_RIGHT)
        start(c, OTHER_ON_RIGHT)
        arrived(c, OTHER_LEFT)
        start(c, OTHER_ON_LEFT)
        arrived(c, LEFT_OVER, RIGHT_OVER)

    pl.semaphore_wait(barrier, len(neighbours))
    issue_zero(0)
    greet(word.at[0])
    for copy in row_loads[1]:
        copy.wait()
    lax.fori_loop(size, freqs, pack, 0, unroll=4)
    trans_load.wait()
    amplitude = trans[...].astype(jnp.float32)
    weight[...] = amplitude * amplitude
    acc[...] = jnp.zeros_like(acc)

    half = lanes
    tri_line = lax.broadcasted_iota(jnp.int32, (half, half), 0)
    tri_column = lax.broadcasted_iota(jnp.int32, (half, half), 1)
    upper = tri_line <= tri_column
    blank = jnp.zeros((half, half), jnp.bfloat16)
    depth2 = field.shape[1] * field.shape[2]
    cells = field.shape[3]

    def block(first, f, part):
        return gathered[pl.ds(first, ring), pl.ds(per_freq * f + 2 * part, 2)].reshape(half, half)

    for slot in range(2):
        for i, j in ((0, 3), (1, 0), (2, 1), (3, 2)):
            matrix[slot, pl.ds(i * half, half), pl.ds(j * half, half)] = blank

    def one_frequency(f, slot):
        def put(i, j, value):
            matrix[slot, pl.ds(i * half, half), pl.ds(j * half, half)] = value

        for b in range(2):
            packed = block(b * ring, f, 0)
            sym = jnp.where(upper, packed, blank)
            skew = jnp.where(upper, blank, packed)
            put(b, b, sym)
            put(2 + b, 2 + b, sym)
            put(2 + b, b, skew)
            put(b, 2 + b, -skew)
        across = block(0, f, 1)
        put(0, 1, across)
        put(2, 3, across)
        below = block(ring, f, 1)
        put(3, 0, below)
        put(1, 2, -below)
        v = field[f].reshape(depth2, cells)
        image = jnp.dot(matrix[slot], v, preferred_element_type=jnp.float32)
        power = jnp.sum((v.astype(jnp.float32) * image).reshape(depth2 // 8, 8, cells), axis=0)
        return power * weight[pl.ds(f, 1), :]

    def compute(c, second):
        if not second:
            arrived(c, FAR_OVER, OTHER_ON_RIGHT, OTHER_ON_LEFT)
            load(c).wait()
        f = c * size + second * 2
        acc[...] += one_frequency(f, 0) + one_frequency(f + 1, 1)

    for c in range(1, AHEAD):
        issue_zero(c)
    pl.semaphore_wait(word.at[0], len(neighbours))
    greet(word.at[1])

    def steps(step, carry):
        ready = jnp.logical_and(step >= THIRD, step - THIRD < CHUNKS)

        @pl.when(ready)
        def _():
            compute(step - THIRD, 0)

        @pl.when(step + AHEAD < CHUNKS)
        def _():
            issue_zero(step + AHEAD)

        @pl.when(step < CHUNKS)
        def _():
            issue_one(step)

        @pl.when(jnp.logical_and(step >= SECOND, step - SECOND < CHUNKS))
        def _():
            issue_two(step - SECOND)

        @pl.when(ready)
        def _():
            compute(step - THIRD, 1)

        return carry

    lax.fori_loop(0, CHUNKS + THIRD, steps, 0)

    pl.semaphore_wait(word.at[1], len(neighbours))

    def spread(ref, me, peer, ssem, rsem):
        n = ref.shape[0]

        def copy(step):
            return pltpu.make_async_remote_copy(
                src_ref=ref.at[me], dst_ref=ref.at[me],
                send_sem=ssem.at[step], recv_sem=rsem.at[step],
                device_id=peer(step), device_id_type=MESH,
            )

        def each(act):
            def one(step, carry):
                act(copy(step))
                return carry

            return lambda: lax.fori_loop(1, n, one, 0)

        return (
            each(lambda c: c.start()), each(lambda c: c.wait_recv()), each(lambda c: c.wait_send())
        )

    def sent(c, carry):
        for kind in table:
            copy_of(c, kind).wait_send()
        return carry

    total = 2.0 / (lax.axis_size("freq") * freqs)
    sums[me_sum] = jnp.sum(acc[...], axis=0, keepdims=True) * total
    go, got, gone = spread(sums, me_sum, sum_peer, sum_send, sum_recv)
    go()
    lax.fori_loop(0, CHUNKS, sent, 0)
    got()
    parts[me_part] = jnp.sum(sums[...], axis=0)
    go_part, got_part, gone_part = spread(parts, me_part, part_peer, part_send, part_recv)
    go_part()
    gone()
    got_part()
    ambiguity = parts[cell * Y_LOW] + parts[cell * Y_LOW + 1]
    everywhere = jnp.sum(parts[...].reshape(n_cell, Y_LOW, cells), axis=1)
    peak = jnp.max(jnp.max(everywhere, axis=0, keepdims=True), axis=1, keepdims=True)
    out_ref[0:1, :] = ambiguity
    out_ref[1:2, :] = ambiguity / jnp.maximum(peak, 1.0)
    gone_part()


def shards(covariance, replica, transmission):
    freqs, _, rows, depth = covariance.shape
    cells = replica.shape[3]
    n_freq, n_cell = lax.axis_size("freq"), lax.axis_size("cell")
    out = pl.pallas_call(
        kernel,
        out_shape=jax.ShapeDtypeStruct((2, cells), jnp.float32),
        in_specs=[pl.BlockSpec(memory_space=pltpu.HBM)] * 3,
        out_specs=pl.BlockSpec(memory_space=pltpu.VMEM),
        scratch_shapes=[
            pltpu.VMEM((freqs, 2, rows, depth // 2), jnp.bfloat16),
            pltpu.VMEM((freqs, rows, depth // 2), jnp.bfloat16),
            pltpu.VMEM((n_cell, freqs * 4, rows // 2, depth // 2), jnp.bfloat16),
            pltpu.VMEM((freqs, 2, depth, cells), jnp.bfloat16),
            pltpu.VMEM((freqs, cells), jnp.bfloat16),
            pltpu.VMEM((freqs, cells), jnp.float32),
            pltpu.VMEM((2, 2 * depth, 2 * depth), jnp.bfloat16),
            pltpu.VMEM((8, cells), jnp.float32),
            pltpu.VMEM((n_freq // Y_LOW, 1, cells), jnp.float32),
            pltpu.VMEM((n_cell * Y_LOW, 1, cells), jnp.float32),
            pltpu.SemaphoreType.DMA((5,)),
            pltpu.SemaphoreType.DMA((CHUNKS,)),
            pltpu.SemaphoreType.DMA((CHUNKS, KINDS)),
            pltpu.SemaphoreType.DMA((CHUNKS, KINDS)),
            pltpu.SemaphoreType.DMA((n_freq // Y_LOW,)),
            pltpu.SemaphoreType.DMA((n_freq // Y_LOW,)),
            pltpu.SemaphoreType.DMA((n_cell * Y_LOW,)),
            pltpu.SemaphoreType.DMA((n_cell * Y_LOW,)),
            pltpu.SemaphoreType.REGULAR((2,)),
        ],
        compiler_params=pltpu.CompilerParams(collective_id=0, has_side_effects=True, vmem_limit_bytes=40 * 2**20),
    )(*[pltpu.with_memory_space_constraint(a, pltpu.HBM) for a in (covariance, replica, transmission)])
    return out[0], out[1]


def solution(mesh):
    return jax.shard_map(
        shards,
        mesh=mesh,
        in_specs=(P("freq", None, "cell", None), P("freq", None, None, "cell"), P("freq", "cell")),
        out_specs=(P("cell"), P("cell")),
        check_vma=False,
    )
```

time: 217 us -> 52.2 us (0.24)
  waiting for transfers between devices: 114 us -> 0 us
  Pallas kernels: 0 us -> 50.9 us
  matrix products: 35.5 us -> 0 us
  other arithmetic: 29.5 us -> 0 us
  blocking collectives: 21.7 us -> 0 us
  between operations: 14.7 us -> 0.64 us
    all_gather x1 -> x0, waiting for transfers between devices: 113 us -> none  [shards(): lax.all_gather(covariance, 'cell', axis=2, tiled=True)]
    pallas_call x0 -> x1, Pallas kernels: none -> 50.9 us  [shards(): pl.pallas_call(kernel, out_shape=jax.ShapeDtypeStruct((2, cells), jnp.flo...]
    dot_general x2 -> x0, matrix products: 35.5 us -> none  [the longest x1 17.7 us: quadratic(): jnp.einsum('fij,fjc->fic', stacked, col_fields[:, 1], preferred_element_t...]
    reduce_sum x3 -> x0, other arithmetic: 27.7 us -> none  [the longest x1 27.6 us: quadratic(): jnp.sum(row_fields[:, 0] * image_re + row_fields[:, 1] * image_im, axis=1)]
    all_to_all x2 -> x0, blocking collectives: 21.7 us -> none  [copy_for_each(): return lax.all_to_all(copies, axis, split_axis=0, concat_axis=0, tiled=True)]
  transfers between devices with their start and end apart: 1 -> 0, of which waited for: 1 -> 0; matrix products, arithmetic and copies ran while one was open for 0% -> 0% of each run, Pallas kernels for 0% -> 0%
where the time goes in v3:
time: 52.2 us; the launch traced here: 52.1 us
  Pallas kernels  50.9 us (98%)
  between operations  0.64 us (1%)
  local copies, waits for them, and re-layouts  0.59 us (1%)
    pallas_call x1, Pallas kernels, shards(): pl.pallas_call(kernel, out_shape=jax.ShapeDtypeStruct((2, cells), jnp.flo...  50.9 us

profile of v3, /device:TPU:1, one launch (start us, length us, event | category | flops | bytes accessed | tf_op | source)
XLA Modules:
  0.0 52.1 jit_solution(15269327162478873680)
XLA Ops:
  0.6 50.9 %shard_map.50 = f32[2,512]{1,0:T(2,128)S(1)} custom-call(bf16[32,2,32,256]{3,2,1,0:T(8,128)(2,1)} %cov_hbm.1, bf16[32,2,256,512]{3,2,1,0:T(8,128)(2,1)} %rep_hbm.1, bf16[32,512]{1,0:T(8,128)(2,1)} %trans_hbm.1), custom_call_target="tpu_custom_call" | custom-call | tf_op jit(solution)/shard_map/pallas_call | solution.py:313
  51.5 0.6 %fusion = (f32[1,512]{1,0:T(1,128)}, f32[1,512]{1,0:T(1,128)}) fusion(f32[2,512]{1,0:T(2,128)S(1)} %shard_map.50), kind=kLoop, calls=%fused_computation | loop fusion | bytes 8192 | tf_op jit(solution)/shard_map/slice | solution.py:341

commit v4 on v3

--- a/solution.py
+++ b/solution.py
@@ -10,18 +10,29 @@
 MESH = pl.DeviceIdType.MESH
 CHUNKS = 8
 PIECES = 16
-BY_X = 9
-AHEAD = 3
-SECOND = 2
-THIRD = 5
-KINDS = 12
+BY_X = 8
+AHEAD = 4
+PROGRAM = (
+    ("over", 0),
+    ("other", 2),
+    ("x", 4),
+    ("cx", 4),
+    ("y", 5),
+    ("far", 2),
+    ("near", 0),
+    ("send", -AHEAD),
+    ("cy", 5),
+)
+PAIRS = {"cx": (0, 1), "cy": (2, 3)}
+FIRST = "cx"
+GROUPS = 6
 CORES, Y_LOW = 2, 2
 
 
 def kernel(
     cov_hbm, rep_hbm, trans_hbm, out_ref,
     diag, far, gathered, field, trans, weight, matrix, acc, sums, parts,
-    load_sem, rep_sem, send_sem, recv_sem, sum_send, sum_recv, part_send, part_recv, word,
+    load_sem, rep_sem, send_sem, recv_sem, sum_sem, part_sem, word,
 ):
     freq, cell = lax.axis_index("freq"), lax.axis_index("cell")
     n_cell = lax.axis_size("cell")
@@ -31,6 +42,39 @@
     def at(shift, other=False):
         r = 1 - row if other else row
         return r * ring + lax.rem(x + shift + ring, ring)
+
+    core, y_low = lax.rem(freq, CORES), lax.rem(lax.div(freq, CORES), Y_LOW)
+    z = lax.div(freq, CORES * Y_LOW)
+    me_sum, n_sum = z * CORES + core, sums.shape[0]
+    me_part, n_part = cell * Y_LOW + y_low, parts.shape[0]
+
+    def sum_peer(step):
+        j = lax.rem(me_sum + step, n_sum)
+        return {"freq": (lax.div(j, CORES) * Y_LOW + y_low) * CORES + lax.rem(j, CORES)}
+
+    def part_peer(step):
+        j = lax.rem(me_part + step, n_part)
+        return {
+            "freq": (z * Y_LOW + lax.rem(j, Y_LOW)) * CORES + core, "cell": lax.div(j, Y_LOW)
+        }
+
+    barrier = pltpu.get_barrier_semaphore()
+
+    n_z = n_sum // CORES
+    freq_at = lambda zz, yy, cc: {"freq": (zz * Y_LOW + yy) * CORES + cc}
+    neighbours = (
+        {"cell": at(1)}, {"cell": at(-1)}, {"cell": at(0, True)},
+        freq_at(z, y_low, 1 - core),
+        freq_at(lax.rem(z + 1, n_z), y_low, core), freq_at(lax.rem(z + n_z - 1, n_z), y_low, core),
+        freq_at(z, 1 - y_low, core),
+        {**freq_at(z, 1 - y_low, core), "cell": at(0, True)},
+    )
+
+    def greet(semaphore):
+        for target in neighbours:
+            pl.semaphore_signal(semaphore, inc=1, device_id=target, device_id_type=MESH)
+
+    greet(barrier)
 
     lanes = gathered.shape[-1]
     freqs = field.shape[0]
@@ -53,46 +97,13 @@
 
     def load(c):
         part = pl.ds(c * size, size)
-        return pltpu.make_async_copy(rep_hbm.at[part], field.at[part], rep_sem.at[c])
+        return pltpu.make_async_copy(rep_hbm.at[part], field.at[part], rep_sem)
 
     def load_one(c, carry):
         load(c).start()
         return carry
 
     lax.fori_loop(0, CHUNKS, load_one, 0)
-
-    core, y_low = lax.rem(freq, CORES), lax.rem(lax.div(freq, CORES), Y_LOW)
-    z = lax.div(freq, CORES * Y_LOW)
-    me_sum, n_sum = z * CORES + core, sums.shape[0]
-    me_part, n_part = cell * Y_LOW + y_low, parts.shape[0]
-
-    def sum_peer(step):
-        j = lax.rem(me_sum + step, n_sum)
-        return {"freq": (lax.div(j, CORES) * Y_LOW + y_low) * CORES + lax.rem(j, CORES)}
-
-    def part_peer(step):
-        j = lax.rem(me_part + step, n_part)
-        return {
-            "freq": (z * Y_LOW + lax.rem(j, Y_LOW)) * CORES + core, "cell": lax.div(j, Y_LOW)
-        }
-
-    barrier = pltpu.get_barrier_semaphore()
-
-    n_z = n_sum // CORES
-    freq_at = lambda zz, yy, cc: {"freq": (zz * Y_LOW + yy) * CORES + cc}
-    neighbours = (
-        {"cell": at(1)}, {"cell": at(-1)}, {"cell": at(0, True)},
-        freq_at(z, y_low, 1 - core),
-        freq_at(lax.rem(z + 1, n_z), y_low, core), freq_at(lax.rem(z + n_z - 1, n_z), y_low, core),
-        freq_at(z, 1 - y_low, core),
-        {**freq_at(z, 1 - y_low, core), "cell": at(0, True)},
-    )
-
-    def greet(semaphore):
-        for target in neighbours:
-            pl.semaphore_signal(semaphore, inc=1, device_id=target, device_id_type=MESH)
-
-    greet(barrier)
 
     shape = diag.shape[2:]
     rows = shape[0] // 2
@@ -134,42 +145,47 @@
         OTHER_ON_LEFT: (at(1, True), left, mid_x, BY_X - mid_x),
     }
 
-    def copy_of(c, kind):
-        source, target, first, count = table[kind]
-        ref = gathered.at[source, pl.ds(c * PIECES + first, count)]
-        return pltpu.make_async_remote_copy(
-            src_ref=ref, dst_ref=ref,
-            send_sem=send_sem.at[c, kind], recv_sem=recv_sem.at[c, kind],
-            device_id={"cell": target}, device_id_type=MESH,
-        )
+    NEAR, OVER, ON, OTHER, BY_Y, LAST = range(6)
+    group = {
+        TO_RIGHT: NEAR, TO_LEFT: NEAR, TO_PARTNER: OVER, ON_RIGHT: ON, ON_LEFT: ON,
+        OTHER_RIGHT: OTHER, OTHER_LEFT: OTHER, LEFT_OVER: BY_Y, RIGHT_OVER: BY_Y,
+        FAR_OVER: BY_Y, OTHER_ON_RIGHT: LAST, OTHER_ON_LEFT: LAST,
+    }
+    landing = {
+        NEAR: (pl.ds(0, 2), 0, PIECES),
+        OVER: (partner, 0, PIECES),
+        ON: (at(2), 0, PIECES),
+        OTHER: (pl.ds(0, 2), 0, BY_X),
+        BY_Y: (pl.ds(0, 3), BY_X, by_y),
+        LAST: (at(2, True), 0, BY_X),
+    }
 
     def start(c, *wanted):
         for kind in wanted:
-            copy_of(c, kind).start()
-
-    def arrived(c, *wanted):
-        for kind in wanted:
-            copy_of(c, kind).wait_recv()
+            source, target, first, count = table[kind]
+            ref = gathered.at[source, pl.ds(c * PIECES + first, count)]
+            pltpu.make_async_remote_copy(
+                src_ref=ref, dst_ref=ref,
+                send_sem=send_sem, recv_sem=recv_sem.at[c, group[kind]],
+                device_id={"cell": target}, device_id_type=MESH,
+            ).start()
+
+    def arrived(c, which):
+        source, first, count = landing[which]
+        ref = gathered.at[source, pl.ds(c * PIECES + first, count)]
+        pltpu.make_async_copy(ref, ref, recv_sem.at[c, which]).wait()
 
     def issue_zero(c):
         start(c, TO_PARTNER, TO_RIGHT, TO_LEFT)
 
-    def issue_one(c):
-        arrived(c, TO_RIGHT)
-        start(c, ON_RIGHT, LEFT_OVER)
-        arrived(c, TO_LEFT)
-        start(c, ON_LEFT, RIGHT_OVER)
-        arrived(c, TO_PARTNER)
-        start(c, OTHER_RIGHT, OTHER_LEFT)
-
-    def issue_two(c):
-        arrived(c, ON_RIGHT, ON_LEFT)
-        start(c, FAR_OVER)
-        arrived(c, OTHER_RIGHT)
-        start(c, OTHER_ON_RIGHT)
-        arrived(c, OTHER_LEFT)
-        start(c, OTHER_ON_LEFT)
-        arrived(c, LEFT_OVER, RIGHT_OVER)
+    actions = {
+        "near": (NEAR, (ON_RIGHT, ON_LEFT, LEFT_OVER, RIGHT_OVER)),
+        "over": (OVER, (OTHER_RIGHT, OTHER_LEFT)),
+        "far": (ON, (FAR_OVER,)),
+        "other": (OTHER, (OTHER_ON_RIGHT, OTHER_ON_LEFT)),
+        "y": (BY_Y, ()),
+        "x": (LAST, ()),
+    }
 
     pl.semaphore_wait(barrier, len(neighbours))
     issue_zero(0)
@@ -220,12 +236,20 @@
         power = jnp.sum((v.astype(jnp.float32) * image).reshape(depth2 // 8, 8, cells), axis=0)
         return power * weight[pl.ds(f, 1), :]
 
-    def compute(c, second):
-        if not second:
-            arrived(c, FAR_OVER, OTHER_ON_RIGHT, OTHER_ON_LEFT)
-            load(c).wait()
-        f = c * size + second * 2
-        acc[...] += one_frequency(f, 0) + one_frequency(f + 1, 1)
+    def act(name, c):
+        if name in PAIRS:
+            if name == FIRST:
+
+                @pl.when(c == 0)
+                def _():
+                    pltpu.make_async_copy(rep_hbm, field, rep_sem).wait()
+
+            f, g = (c * size + offset for offset in PAIRS[name])
+            acc[...] += one_frequency(f, 0) + one_frequency(g, 1)
+            return
+        which, starts = actions[name]
+        arrived(c, which)
+        start(c, *starts)
 
     for c in range(1, AHEAD):
         issue_zero(c)
@@ -233,77 +257,50 @@
     greet(word.at[1])
 
     def steps(step, carry):
-        ready = jnp.logical_and(step >= THIRD, step - THIRD < CHUNKS)
-
-        @pl.when(ready)
-        def _():
-            compute(step - THIRD, 0)
-
-        @pl.when(step + AHEAD < CHUNKS)
-        def _():
-            issue_zero(step + AHEAD)
-
-        @pl.when(step < CHUNKS)
-        def _():
-            issue_one(step)
-
-        @pl.when(jnp.logical_and(step >= SECOND, step - SECOND < CHUNKS))
-        def _():
-            issue_two(step - SECOND)
-
-        @pl.when(ready)
-        def _():
-            compute(step - THIRD, 1)
-
+        for name, lag in PROGRAM:
+            c = step - lag
+            if name == "send":
+                pl.when(c < CHUNKS)(functools.partial(issue_zero, c))
+            else:
+                inside = jnp.logical_and(c >= 0, c < CHUNKS)
+                pl.when(inside)(functools.partial(act, name, c))
         return carry
 
-    lax.fori_loop(0, CHUNKS + THIRD, steps, 0)
+    lax.fori_loop(0, CHUNKS + max(lag for _, lag in PROGRAM), steps, 0)
 
     pl.semaphore_wait(word.at[1], len(neighbours))
 
     def spread(ref, me, peer, ssem, rsem):
         n = ref.shape[0]
 
-        def copy(step):
-            return pltpu.make_async_remote_copy(
-                src_ref=ref.at[me], dst_ref=ref.at[me],
-                send_sem=ssem.at[step], recv_sem=rsem.at[step],
+        def one(step, carry):
+            pltpu.make_async_remote_copy(
+                src_ref=ref.at[me], dst_ref=ref.at[me], send_sem=ssem, recv_sem=rsem,
                 device_id=peer(step), device_id_type=MESH,
-            )
-
-        def each(act):
-            def one(step, carry):
-                act(copy(step))
-                return carry
-
-            return lambda: lax.fori_loop(1, n, one, 0)
-
-        return (
-            each(lambda c: c.start()), each(lambda c: c.wait_recv()), each(lambda c: c.wait_send())
-        )
-
-    def sent(c, carry):
-        for kind in table:
-            copy_of(c, kind).wait_send()
-        return carry
+            ).start()
+            return carry
+
+        lax.fori_loop(1, n, one, 0)
+
+    def all_but_one(ref, semaphore):
+        part = ref.at[pl.ds(0, ref.shape[0] - 1)]
+        pltpu.make_async_copy(part, part, semaphore).wait()
 
     total = 2.0 / (lax.axis_size("freq") * freqs)
     sums[me_sum] = jnp.sum(acc[...], axis=0, keepdims=True) * total
-    go, got, gone = spread(sums, me_sum, sum_peer, sum_send, sum_recv)
-    go()
-    lax.fori_loop(0, CHUNKS, sent, 0)
-    got()
+    spread(sums, me_sum, sum_peer, sum_sem.at[0], sum_sem.at[1])
+    all_but_one(gathered, send_sem)
+    all_but_one(sums, sum_sem.at[1])
     parts[me_part] = jnp.sum(sums[...], axis=0)
-    go_part, got_part, gone_part = spread(parts, me_part, part_peer, part_send, part_recv)
-    go_part()
-    gone()
-    got_part()
+    spread(parts, me_part, part_peer, part_sem.at[0], part_sem.at[1])
+    all_but_one(sums, sum_sem.at[0])
+    all_but_one(parts, part_sem.at[1])
     ambiguity = parts[cell * Y_LOW] + parts[cell * Y_LOW + 1]
     everywhere = jnp.sum(parts[...].reshape(n_cell, Y_LOW, cells), axis=1)
     peak = jnp.max(jnp.max(everywhere, axis=0, keepdims=True), axis=1, keepdims=True)
     out_ref[0:1, :] = ambiguity
     out_ref[1:2, :] = ambiguity / jnp.maximum(peak, 1.0)
-    gone_part()
+    all_but_one(parts, part_sem.at[0])
 
 
 def shards(covariance, replica, transmission):
@@ -327,13 +324,11 @@
             pltpu.VMEM((n_freq // Y_LOW, 1, cells), jnp.float32),
             pltpu.VMEM((n_cell * Y_LOW, 1, cells), jnp.float32),
             pltpu.SemaphoreType.DMA((5,)),
-            pltpu.SemaphoreType.DMA((CHUNKS,)),
-            pltpu.SemaphoreType.DMA((CHUNKS, KINDS)),
-            pltpu.SemaphoreType.DMA((CHUNKS, KINDS)),
-            pltpu.SemaphoreType.DMA((n_freq // Y_LOW,)),
-            pltpu.SemaphoreType.DMA((n_freq // Y_LOW,)),
-            pltpu.SemaphoreType.DMA((n_cell * Y_LOW,)),
-            pltpu.SemaphoreType.DMA((n_cell * Y_LOW,)),
+            pltpu.SemaphoreType.DMA,
+            pltpu.SemaphoreType.DMA,
+            pltpu.SemaphoreType.DMA((CHUNKS, GROUPS)),
+            pltpu.SemaphoreType.DMA((2,)),
+            pltpu.SemaphoreType.DMA((2,)),
             pltpu.SemaphoreType.REGULAR((2,)),
         ],
         compiler_params=pltpu.CompilerParams(collective_id=0, has_side_effects=True, vmem_limit_bytes=40 * 2**20),

time: 52.2 us -> 49.2 us (0.943)
  Pallas kernels: 50.9 us -> 47.8 us
    pallas_call x1, Pallas kernels: 50.9 us -> 47.8 us  [shards(): pl.pallas_call(kernel, out_shape=jax.ShapeDtypeStruct((2, cells), jnp.flo...]
where the time goes in v4:
time: 49.2 us; the launch traced here: 49.1 us
  Pallas kernels  47.8 us (97%)
  between operations  0.64 us (1%)
  local copies, waits for them, and re-layouts  0.59 us (1%)
    pallas_call x1, Pallas kernels, shards(): pl.pallas_call(kernel, out_shape=jax.ShapeDtypeStruct((2, cells), jnp.flo...  47.8 us

profile of v4, /device:TPU:1, one launch (start us, length us, event | category | flops | bytes accessed | tf_op | source)
XLA Modules:
  0.0 49.1 jit_solution(3355117594970505495)
XLA Ops:
  0.6 47.8 %shard_map.50 = f32[2,512]{1,0:T(2,128)S(1)} custom-call(bf16[32,2,32,256]{3,2,1,0:T(8,128)(2,1)} %cov_hbm.1, bf16[32,2,256,512]{3,2,1,0:T(8,128)(2,1)} %rep_hbm.1, bf16[32,512]{1,0:T(8,128)(2,1)} %trans_hbm.1), custom_call_target="tpu_custom_call" | custom-call | tf_op jit(solution)/shard_map/pallas_call | solution.py:310
  48.5 0.6 %fusion = (f32[1,512]{1,0:T(1,128)}, f32[1,512]{1,0:T(1,128)}) fusion(f32[2,512]{1,0:T(2,128)S(1)} %shard_map.50), kind=kLoop, calls=%fused_computation | loop fusion | bytes 8192 | tf_op jit(solution)/shard_map/slice | solution.py:336

commit v5 on v4

--- a/solution.py
+++ b/solution.py
@@ -76,6 +76,12 @@
 
     greet(barrier)
 
+    def slot(shift, other=False):
+        r, to = 1 - row if other else row, lax.rem(x + shift + ring, ring)
+        return r * ring + lax.rem(to, 2) * (ring // 2) + lax.div(to, 2)
+
+    beside = row * ring + (1 - lax.rem(x, 2)) * (ring // 2)
+
     lanes = gathered.shape[-1]
     freqs = field.shape[0]
     per_freq = gathered.shape[1] // freqs
@@ -116,8 +122,8 @@
         packed = jnp.where(above, diag[f, 0] * factor, diag[f, 1])
         across = far[f]
         for i in range(2):
-            gathered[cell, per_freq * f + i] = packed[i * rows:(i + 1) * rows]
-            gathered[cell, per_freq * f + 2 + i] = across[i * rows:(i + 1) * rows]
+            gathered[slot(0), per_freq * f + i] = packed[i * rows:(i + 1) * rows]
+            gathered[slot(0), per_freq * f + 2 + i] = across[i * rows:(i + 1) * rows]
         return carry
 
     for copy in row_loads[0]:
@@ -125,48 +131,39 @@
     lax.fori_loop(0, size, pack, 0, unroll=4)
 
     right, left, partner = at(1), at(-1), at(0, True)
-    TO_PARTNER, TO_RIGHT, TO_LEFT = 0, 1, 2
-    ON_RIGHT, LEFT_OVER, ON_LEFT, RIGHT_OVER, OTHER_RIGHT, OTHER_LEFT = 3, 4, 5, 6, 7, 8
-    FAR_OVER, OTHER_ON_RIGHT, OTHER_ON_LEFT = 9, 10, 11
-
+    TO_PARTNER, TO_RIGHT, TO_LEFT, ON_RIGHT, ON_LEFT, BOTH_OVER = range(6)
+    OTHER_RIGHT, OTHER_LEFT, FAR_OVER, OTHER_ON_RIGHT, OTHER_ON_LEFT = range(6, 11)
+    NEAR, OVER, ON, OTHER, BY_Y, LAST = range(GROUPS)
     mid, mid_x, by_y = PIECES // 2, BY_X // 2, PIECES - BY_X
     table = {
-        TO_PARTNER: (cell, partner, 0, PIECES),
-        TO_RIGHT: (cell, right, 0, PIECES),
-        TO_LEFT: (cell, left, 0, PIECES),
-        ON_RIGHT: (left, right, 0, mid),
-        LEFT_OVER: (left, partner, BY_X, by_y),
-        ON_LEFT: (right, left, mid, PIECES - mid),
-        RIGHT_OVER: (right, partner, BY_X, by_y),
-        OTHER_RIGHT: (partner, right, 0, BY_X),
-        OTHER_LEFT: (partner, left, 0, BY_X),
-        FAR_OVER: (at(2), partner, BY_X, by_y),
-        OTHER_ON_RIGHT: (at(-1, True), right, 0, mid_x),
-        OTHER_ON_LEFT: (at(1, True), left, mid_x, BY_X - mid_x),
-    }
-
-    NEAR, OVER, ON, OTHER, BY_Y, LAST = range(6)
-    group = {
-        TO_RIGHT: NEAR, TO_LEFT: NEAR, TO_PARTNER: OVER, ON_RIGHT: ON, ON_LEFT: ON,
-        OTHER_RIGHT: OTHER, OTHER_LEFT: OTHER, LEFT_OVER: BY_Y, RIGHT_OVER: BY_Y,
-        FAR_OVER: BY_Y, OTHER_ON_RIGHT: LAST, OTHER_ON_LEFT: LAST,
+        TO_PARTNER: (slot(0), partner, 0, PIECES, OVER),
+        TO_RIGHT: (slot(0), right, 0, PIECES, NEAR),
+        TO_LEFT: (slot(0), left, 0, PIECES, NEAR),
+        ON_RIGHT: (slot(-1), right, 0, mid, ON),
+        ON_LEFT: (slot(1), left, mid, PIECES - mid, ON),
+        BOTH_OVER: (pl.ds(beside, 2), partner, BY_X, by_y, BY_Y),
+        OTHER_RIGHT: (slot(0, True), right, 0, BY_X, OTHER),
+        OTHER_LEFT: (slot(0, True), left, 0, BY_X, OTHER),
+        FAR_OVER: (slot(2), partner, BY_X, by_y, BY_Y),
+        OTHER_ON_RIGHT: (slot(-1, True), right, 0, mid_x, LAST),
+        OTHER_ON_LEFT: (slot(1, True), left, mid_x, BY_X - mid_x, LAST),
     }
     landing = {
         NEAR: (pl.ds(0, 2), 0, PIECES),
-        OVER: (partner, 0, PIECES),
-        ON: (at(2), 0, PIECES),
+        OVER: (slot(0, True), 0, PIECES),
+        ON: (slot(2), 0, PIECES),
         OTHER: (pl.ds(0, 2), 0, BY_X),
         BY_Y: (pl.ds(0, 3), BY_X, by_y),
-        LAST: (at(2, True), 0, BY_X),
+        LAST: (slot(2, True), 0, BY_X),
     }
 
     def start(c, *wanted):
         for kind in wanted:
-            source, target, first, count = table[kind]
+            source, target, first, count, group = table[kind]
             ref = gathered.at[source, pl.ds(c * PIECES + first, count)]
             pltpu.make_async_remote_copy(
                 src_ref=ref, dst_ref=ref,
-                send_sem=send_sem, recv_sem=recv_sem.at[c, group[kind]],
+                send_sem=send_sem, recv_sem=recv_sem.at[c, group],
                 device_id={"cell": target}, device_id_type=MESH,
             ).start()
 
@@ -179,7 +176,7 @@
         start(c, TO_PARTNER, TO_RIGHT, TO_LEFT)
 
     actions = {
-        "near": (NEAR, (ON_RIGHT, ON_LEFT, LEFT_OVER, RIGHT_OVER)),
+        "near": (NEAR, (ON_RIGHT, ON_LEFT, BOTH_OVER)),
         "over": (OVER, (OTHER_RIGHT, OTHER_LEFT)),
         "far": (ON, (FAR_OVER,)),
         "other": (OTHER, (OTHER_ON_RIGHT, OTHER_ON_LEFT)),
@@ -207,7 +204,11 @@
     cells = field.shape[3]
 
     def block(first, f, part):
-        return gathered[pl.ds(first, ring), pl.ds(per_freq * f + 2 * part, 2)].reshape(half, half)
+        pieces = pl.ds(per_freq * f + 2 * part, 2)
+        order = [first + to % 2 * (ring // 2) + to // 2 for to in range(ring)]
+        return jnp.concatenate(
+            [gathered[i, pieces].reshape(half // ring, half) for i in order]
+        )
 
     for slot in range(2):
         for i, j in ((0, 3), (1, 0), (2, 1), (3, 2)):
@@ -253,10 +254,13 @@
 
     for c in range(1, AHEAD):
         issue_zero(c)
-    pl.semaphore_wait(word.at[0], len(neighbours))
-    greet(word.at[1])
 
     def steps(step, carry):
+        @pl.when(step == 3)
+        def _():
+            pl.semaphore_wait(word.at[0], len(neighbours))
+            greet(word.at[1])
+
         for name, lag in PROGRAM:
             c = step - lag
             if name == "send":

time: 49.2 us -> 49.2 us (level)
  no operation moved by 1% of the time
where the time goes in v5:
time: 49.2 us; the launch traced here: 49.1 us
  Pallas kernels  47.9 us (97%)
  between operations  0.64 us (1%)
  local copies, waits for them, and re-layouts  0.59 us (1%)
    pallas_call x1, Pallas kernels, shards(): pl.pallas_call(kernel, out_shape=jax.ShapeDtypeStruct((2, cells), jnp.flo...  47.9 us

profile of v5, /device:TPU:1, one launch (start us, length us, event | category | flops | bytes accessed | tf_op | source)
XLA Modules:
  0.0 49.1 jit_solution(9515742124168220232)
XLA Ops:
  0.6 47.9 %shard_map.50 = f32[2,512]{1,0:T(2,128)S(1)} custom-call(bf16[32,2,32,256]{3,2,1,0:T(8,128)(2,1)} %cov_hbm.1, bf16[32,2,256,512]{3,2,1,0:T(8,128)(2,1)} %rep_hbm.1, bf16[32,512]{1,0:T(8,128)(2,1)} %trans_hbm.1), custom_call_target="tpu_custom_call" | custom-call | tf_op jit(solution)/shard_map/pallas_call | solution.py:314
  48.5 0.6 %fusion = (f32[1,512]{1,0:T(1,128)}, f32[1,512]{1,0:T(1,128)}) fusion(f32[2,512]{1,0:T(2,128)S(1)} %shard_map.50), kind=kLoop, calls=%fused_computation | loop fusion | bytes 8192 | tf_op jit(solution)/shard_map/slice | solution.py:340

commit v6 on v5

--- a/solution.py
+++ b/solution.py
@@ -17,10 +17,10 @@
     ("other", 2),
     ("x", 4),
     ("cx", 4),
-    ("y", 5),
     ("far", 2),
     ("near", 0),
     ("send", -AHEAD),
+    ("y", 5),
     ("cy", 5),
 )
 PAIRS = {"cx": (0, 1), "cy": (2, 3)}

time: 49.2 us -> 49.2 us (level)
  no operation moved by 1% of the time
where the time goes in v6:
time: 49.2 us; the launch traced here: 49.1 us
  Pallas kernels  47.9 us (97%)
  between operations  0.64 us (1%)
  local copies, waits for them, and re-layouts  0.59 us (1%)
    pallas_call x1, Pallas kernels, shards(): pl.pallas_call(kernel, out_shape=jax.ShapeDtypeStruct((2, cells), jnp.flo...  47.9 us

profile of v6, /device:TPU:1, one launch (start us, length us, event | category | flops | bytes accessed | tf_op | source)
XLA Modules:
  0.0 49.1 jit_solution(7777245574217833355)
XLA Ops:
  0.6 47.9 %shard_map.50 = f32[2,512]{1,0:T(2,128)S(1)} custom-call(bf16[32,2,32,256]{3,2,1,0:T(8,128)(2,1)} %cov_hbm.1, bf16[32,2,256,512]{3,2,1,0:T(8,128)(2,1)} %rep_hbm.1, bf16[32,512]{1,0:T(8,128)(2,1)} %trans_hbm.1), custom_call_target="tpu_custom_call" | custom-call | tf_op jit(solution)/shard_map/pallas_call | solution.py:314
  48.5 0.6 %fusion = (f32[1,512]{1,0:T(1,128)}, f32[1,512]{1,0:T(1,128)}) fusion(f32[2,512]{1,0:T(2,128)S(1)} %shard_map.50), kind=kLoop, calls=%fused_computation | loop fusion | bytes 8192 | tf_op jit(solution)/shard_map/slice | solution.py:340
